TPU v7x, 32 devices: a whole 2x2x4 slice. The times are simulated.
32 devices in a mesh: mkt: 8 (over y, x, core), trade: 1, scen: 4 (over z).
Axes of the slice: x: 2, y: 2, z: 4, core: 2. Of those that a mesh axis runs over, the one named last changes fastest.
Arguments:
- quotes: bfloat16 [512, 512], P('mkt'), may hold values from -6 to 6
- kernel: bfloat16 [64, 128, 128], P(('trade', 'scen')), may hold values from -0.5 to 0.5
- trade_block: int32 [2048], P('trade'), may hold values from 0 to 63
- trade_embed: bfloat16 [2048, 256], P('trade'), may hold values from -6 to 6
- position: float32 [2048], P('trade'), may hold values from -0.125 to 0.125
- scen_rank: int32 [512], P(('mkt', 'scen')), may hold values from 0 to 511, each once
- w_in: bfloat16 [128, 256], replicated, may hold values from -0.5 to 0.5
- w_mid: bfloat16 [256, 256], replicated, may hold values from -0.375 to 0.375
- b_mid: float32 [256], replicated, may hold values from -6 to 6
- w_out: bfloat16 [256], replicated, may hold values from -0.375 to 0.375
Outputs:
- book_pnl: float32 [512], P(('mkt', 'scen'))
- marginal: float32 [2048], P('trade')
- shortfall: float32 [], replicated
Inputs may be any that keep to these rules, and one draw needn't show every extreme that they name: scen_rank holds each rank of 0 to 511 once.
All inputs are finite; a program needn't handle non-finite values.
Results may differ from a plain program's by a relative error of at most 0.014.
The roundings to bfloat16 on the way count: a program that leaves them out, or rounds other values in their place, can miss the bound.
Values may be sent and summed in bfloat16 or wider, within the bound.
No kernel may reach another device: no remote copies, remote signals or barrier semaphores. Data moves between devices by JAX's collectives and lax.ppermute only.
A program may use at most 64 MiB of HBM per device.

v0:
```python
import jax
import jax.numpy as jnp
from jax import lax
from jax.sharding import PartitionSpec as P

SEG = 128
WIN = 128
QSTEP = 8


def local(quotes, kernel, trade_block, trade_embed, position, scen_rank, w_in, w_mid, b_mid, w_out):
    local_count = kernel.shape[0]
    quote_count = quotes.shape[1]
    row_count = quotes.shape[0]
    first_block = lax.axis_index(("trade", "scen")) * local_count

    def cut_window(local_block):
        block_index = first_block + local_block
        window_start = jnp.clip(QSTEP * block_index - (WIN - QSTEP) // 2, 0, quote_count - WIN)
        return lax.dynamic_slice_in_dim(quotes, window_start, WIN, 1)

    windows = jax.vmap(cut_window)(jnp.arange(local_count, dtype=jnp.int32))
    built_state = jnp.einsum("jrw,jws->jrs", windows, kernel, preferred_element_type=jnp.float32)
    built_state = built_state.astype(jnp.bfloat16).reshape(local_count, row_count * SEG)
    scen_count = scen_rank.shape[0]
    quarter = lax.all_to_all(built_state, "scen", split_axis=1, concat_axis=0, tiled=True)
    table = lax.all_gather(quarter, "trade", axis=0, tiled=True)
    trade_rows_all = table[trade_block]
    embed_float = trade_embed.astype(jnp.float32)

    def price(scen_index):
        trade_rows = lax.dynamic_slice_in_dim(trade_rows_all, scen_index * SEG, SEG, 1)
        hidden_one = jax.nn.silu(
            jnp.dot(trade_rows, w_in, preferred_element_type=jnp.float32) + embed_float
        ).astype(jnp.bfloat16)
        hidden_two = jax.nn.silu(
            jnp.dot(hidden_one, w_mid, preferred_element_type=jnp.float32) + b_mid
        ).astype(jnp.bfloat16)
        return jnp.dot(hidden_two, w_out, preferred_element_type=jnp.float32)

    values = lax.map(price, jnp.arange(scen_count, dtype=jnp.int32))
    scen_total = scen_count * lax.axis_size("mkt") * lax.axis_size("scen")
    decay_span = scen_total // 20
    weight_sum = jnp.sum(jnp.exp(-jnp.arange(scen_total, dtype=jnp.float32) / decay_span))
    weights = jnp.exp(-scen_rank.astype(jnp.float32) / decay_span) / weight_sum
    pnl_part = jnp.dot(values, position, precision=lax.Precision.HIGHEST)
    marginal = lax.psum(-jnp.dot(weights, values, precision=lax.Precision.HIGHEST), ("mkt", "scen"))
    book_pnl = lax.psum(pnl_part, "trade")
    local_tail = -jnp.dot(weights, book_pnl, precision=lax.Precision.HIGHEST)
    shortfall = lax.psum(local_tail, ("mkt", "scen"))
    return (book_pnl, marginal, shortfall)


def solution(mesh):
    placed = (
        P("mkt", None),
        P(("trade", "scen"), None, None),
        P("trade"),
        P("trade", None),
        P("trade"),
        P(("mkt", "scen")),
        P(),
        P(),
        P(),
        P(),
    )
    return jax.shard_map(
        local,
        mesh=mesh,
        in_specs=placed,
        out_specs=(P(("mkt", "scen")), P("trade"), P()),
        check_vma=False,
    )
```

profile of v0, /device:TPU:0, one launch (start us, length us, event | category | flops | bytes accessed | tf_op | source)
XLA Modules:
  0.0 204.2 jit_solution(12396054698393962323)
XLA Ops:
  0.7 33.3 %while.12 = (s32[]{:T(128)}, bf16[64,512]{1,0:T(8,128)(2,1)}, s32[16,2]{0,1:T(2,128)S(1)}, bf16[16,64,128]{2,1,0:T(8,128)(2,1)S(1)}, s32[]{:T(128)}) while((s32[]{:T(128)}, bf16[64,512]{1,0:T(8,128)(2,1)}, s32[16,2]{0,1:T(2,128)S(1)}, bf16[16,64,128]{2,1,0:T(8,128)(2,1)S(1)}, s32[]{:T(128)}) %tuple.34), condition=%wide.while_cond, body=%wide.while_body.sunk | while | flops 2 | bytes 32865 | solution.py:20
  35.2 6.0 %all-to-all-start = ((bf16[16,4,2048]{2,0,1:T(8,128)(2,1)}), bf16[16,4,2048]{2,0,1:T(8,128)(2,1)S(1)}, u32[]{:S(2)}, u32[]{:S(2)}) async-start(bf16[16,4,2048]{2,0,1:T(8,128)(2,1)} %copy.14), calls=%async_computation | async-start | bytes 524288 | tf_op jit(solution)/shard_map/all_to_all | solution.py:26
  43.2 6.9 %all-to-all-done = bf16[16,4,2048]{2,0,1:T(8,128)(2,1)S(1)} async-done(((bf16[16,4,2048]{2,0,1:T(8,128)(2,1)}), bf16[16,4,2048]{2,0,1:T(8,128)(2,1)S(1)}, u32[]{:S(2)}, u32[]{:S(2)}) %all-to-all-start) | async-done | bytes 262176 | tf_op jit(solution)/shard_map/all_to_all | solution.py:26
  50.2 11.0 %gather_fusion = bf16[2048,2048]{1,0:T(8,128)(2,1)} fusion(bf16[64,2048]{1,0:T(8,128)(2,1)S(1)} %bitcast.38, s32[2048]{0:T(1024)S(1)} %fusion.6), kind=kCustom, calls=%fused_computation | custom fusion | bytes 16785408 | tf_op jit(solution)/shard_map/gather | solution.py:28
  61.2 100.5 %while.11 = (s32[]{:T(128)}, f32[16,2048]{1,0:T(8,128)S(1)}, s32[16]{0:T(128)S(1)}, bf16[2048,2048]{1,0:T(8,128)(2,1)}, bf16[128,256]{1,0:T(8,128)(2,1)S(1)}, /*...) while((s32[]{:T(128)}, f32[16,2048]{1,0:T(8,128)S(1)}, ...), condition=%wide.region_1.2_spmd, body=%wide.region_0.1_spmd.sunk | while | flops 409993216 | bytes 4942527 | solution.py:41
  62.4 2.8 %multiply_convert_fusion.3 = bf16[2048,256]{1,0:T(8,128)(2,1)} fusion(f32[2048,256]{1,0:T(8,128)S(1)} %get-tuple-element.215, bf16[128,256]{1,0:T(8,128)(2,1)S(1)} %get-tuple-element.214, bf16[2048,2048]{1,0:T(8,128)(2,1)} %get-tuple-element.213, s32[]{:T(128)S(6)} %select_n.23), kind=kOutput, calls=%fused_computation.4.clone.1 | convolution fusion | flops 137363456 | bytes 3735556 | tf_op jit(solution)/shard_map/while/body/eval_jaxpr/dot_general | solution.py:34
  65.2 2.0 %fusion.29 = f32[1,2048]{1,0:T(1,128)S(1)} fusion(bf16[256,1]{0,1:T(2,128)(2,1)S(1)} %reshape.77, bf16[2048,256]{1,0:T(8,128)(2,1)} %multiply_convert_fusion.3, bf16[256,256]{1,0:T(8,128)(2,1)S(1)} %get-tuple-element.216, f32[256]{0:T(256)S(1)} %get-tuple-element.217), kind=kOutput, calls=%fused_computation.5.clone.1 | convolution fusion | flops 272629760 | bytes 1189376 | tf_op jit(solution)/shard_map/while/body/eval_jaxpr/dot_general | solution.py:39
  68.7 2.8 %multiply_convert_fusion.3 = bf16[2048,256]{1,0:T(8,128)(2,1)} fusion(f32[2048,256]{1,0:T(8,128)S(1)} %get-tuple-element.215, bf16[128,256]{1,0:T(8,128)(2,1)S(1)} %get-tuple-element.214, bf16[2048,2048]{1,0:T(8,128)(2,1)} %get-tuple-element.213, s32[]{:T(128)S(6)} %select_n.23), kind=kOutput, calls=%fused_computation.4.clone.1 | convolution fusion | flops 137363456 | bytes 3735556 | tf_op jit(solution)/shard_map/while/body/eval_jaxpr/dot_general | solution.py:34
  71.5 2.0 %fusion.29 = f32[1,2048]{1,0:T(1,128)S(1)} fusion(bf16[256,1]{0,1:T(2,128)(2,1)S(1)} %reshape.77, bf16[2048,256]{1,0:T(8,128)(2,1)} %multiply_convert_fusion.3, bf16[256,256]{1,0:T(8,128)(2,1)S(1)} %get-tuple-element.216, f32[256]{0:T(256)S(1)} %get-tuple-element.217), kind=kOutput, calls=%fused_computation.5.clone.1 | convolution fusion | flops 272629760 | bytes 1189376 | tf_op jit(solution)/shard_map/while/body/eval_jaxpr/dot_general | solution.py:39
  75.0 2.8 %multiply_convert_fusion.3 = bf16[2048,256]{1,0:T(8,128)(2,1)} fusion(f32[2048,256]{1,0:T(8,128)S(1)} %get-tuple-element.215, bf16[128,256]{1,0:T(8,128)(2,1)S(1)} %get-tuple-element.214, bf16[2048,2048]{1,0:T(8,128)(2,1)} %get-tuple-element.213, s32[]{:T(128)S(6)} %select_n.23), kind=kOutput, calls=%fused_computation.4.clone.1 | convolution fusion | flops 137363456 | bytes 3735556 | tf_op jit(solution)/shard_map/while/body/eval_jaxpr/dot_general | solution.py:34
  81.3 2.8 %multiply_convert_fusion.3 = bf16[2048,256]{1,0:T(8,128)(2,1)} fusion(f32[2048,256]{1,0:T(8,128)S(1)} %get-tuple-element.215, bf16[128,256]{1,0:T(8,128)(2,1)S(1)} %get-tuple-element.214, bf16[2048,2048]{1,0:T(8,128)(2,1)} %get-tuple-element.213, s32[]{:T(128)S(6)} %select_n.23), kind=kOutput, calls=%fused_computation.4.clone.1 | convolution fusion | flops 137363456 | bytes 3735556 | tf_op jit(solution)/shard_map/while/body/eval_jaxpr/dot_general | solution.py:34
  87.6 2.8 %multiply_convert_fusion.3 = bf16[2048,256]{1,0:T(8,128)(2,1)} fusion(f32[2048,256]{1,0:T(8,128)S(1)} %get-tuple-element.215, bf16[128,256]{1,0:T(8,128)(2,1)S(1)} %get-tuple-element.214, bf16[2048,2048]{1,0:T(8,128)(2,1)} %get-tuple-element.213, s32[]{:T(128)S(6)} %select_n.23), kind=kOutput, calls=%fused_computation.4.clone.1 | convolution fusion | flops 137363456 | bytes 3735556 | tf_op jit(solution)/shard_map/while/body/eval_jaxpr/dot_general | solution.py:34
  93.8 2.8 %multiply_convert_fusion.3 = bf16[2048,256]{1,0:T(8,128)(2,1)} fusion(f32[2048,256]{1,0:T(8,128)S(1)} %get-tuple-element.215, bf16[128,256]{1,0:T(8,128)(2,1)S(1)} %get-tuple-element.214, bf16[2048,2048]{1,0:T(8,128)(2,1)} %get-tuple-element.213, s32[]{:T(128)S(6)} %select_n.23), kind=kOutput, calls=%fused_computation.4.clone.1 | convolution fusion | flops 137363456 | bytes 3735556 | tf_op jit(solution)/shard_map/while/body/eval_jaxpr/dot_general | solution.py:34
  100.1 2.8 %multiply_convert_fusion.3 = bf16[2048,256]{1,0:T(8,128)(2,1)} fusion(f32[2048,256]{1,0:T(8,128)S(1)} %get-tuple-element.215, bf16[128,256]{1,0:T(8,128)(2,1)S(1)} %get-tuple-element.214, bf16[2048,2048]{1,0:T(8,128)(2,1)} %get-tuple-element.213, s32[]{:T(128)S(6)} %select_n.23), kind=kOutput, calls=%fused_computation.4.clone.1 | convolution fusion | flops 137363456 | bytes 3735556 | tf_op jit(solution)/shard_map/while/body/eval_jaxpr/dot_general | solution.py:34
  106.4 2.8 %multiply_convert_fusion.3 = bf16[2048,256]{1,0:T(8,128)(2,1)} fusion(f32[2048,256]{1,0:T(8,128)S(1)} %get-tuple-element.215, bf16[128,256]{1,0:T(8,128)(2,1)S(1)} %get-tuple-element.214, bf16[2048,2048]{1,0:T(8,128)(2,1)} %get-tuple-element.213, s32[]{:T(128)S(6)} %select_n.23), kind=kOutput, calls=%fused_computation.4.clone.1 | convolution fusion | flops 137363456 | bytes 3735556 | tf_op jit(solution)/shard_map/while/body/eval_jaxpr/dot_general | solution.py:34
  112.7 2.8 %multiply_convert_fusion.3 = bf16[2048,256]{1,0:T(8,128)(2,1)} fusion(f32[2048,256]{1,0:T(8,128)S(1)} %get-tuple-element.215, bf16[128,256]{1,0:T(8,128)(2,1)S(1)} %get-tuple-element.214, bf16[2048,2048]{1,0:T(8,128)(2,1)} %get-tuple-element.213, s32[]{:T(128)S(6)} %select_n.23), kind=kOutput, calls=%fused_computation.4.clone.1 | convolution fusion | flops 137363456 | bytes 3735556 | tf_op jit(solution)/shard_map/while/body/eval_jaxpr/dot_general | solution.py:34
  119.0 2.8 %multiply_convert_fusion.3 = bf16[2048,256]{1,0:T(8,128)(2,1)} fusion(f32[2048,256]{1,0:T(8,128)S(1)} %get-tuple-element.215, bf16[128,256]{1,0:T(8,128)(2,1)S(1)} %get-tuple-element.214, bf16[2048,2048]{1,0:T(8,128)(2,1)} %get-tuple-element.213, s32[]{:T(128)S(6)} %select_n.23), kind=kOutput, calls=%fused_computation.4.clone.1 | convolution fusion | flops 137363456 | bytes 3735556 | tf_op jit(solution)/shard_map/while/body/eval_jaxpr/dot_general | solution.py:34
  125.2 2.8 %multiply_convert_fusion.3 = bf16[2048,256]{1,0:T(8,128)(2,1)} fusion(f32[2048,256]{1,0:T(8,128)S(1)} %get-tuple-element.215, bf16[128,256]{1,0:T(8,128)(2,1)S(1)} %get-tuple-element.214, bf16[2048,2048]{1,0:T(8,128)(2,1)} %get-tuple-element.213, s32[]{:T(128)S(6)} %select_n.23), kind=kOutput, calls=%fused_computation.4.clone.1 | convolution fusion | flops 137363456 | bytes 3735556 | tf_op jit(solution)/shard_map/while/body/eval_jaxpr/dot_general | solution.py:34
  131.5 2.8 %multiply_convert_fusion.3 = bf16[2048,256]{1,0:T(8,128)(2,1)} fusion(f32[2048,256]{1,0:T(8,128)S(1)} %get-tuple-element.215, bf16[128,256]{1,0:T(8,128)(2,1)S(1)} %get-tuple-element.214, bf16[2048,2048]{1,0:T(8,128)(2,1)} %get-tuple-element.213, s32[]{:T(128)S(6)} %select_n.23), kind=kOutput, calls=%fused_computation.4.clone.1 | convolution fusion | flops 137363456 | bytes 3735556 | tf_op jit(solution)/shard_map/while/body/eval_jaxpr/dot_general | solution.py:34
  137.8 2.8 %multiply_convert_fusion.3 = bf16[2048,256]{1,0:T(8,128)(2,1)} fusion(f32[2048,256]{1,0:T(8,128)S(1)} %get-tuple-element.215, bf16[128,256]{1,0:T(8,128)(2,1)S(1)} %get-tuple-element.214, bf16[2048,2048]{1,0:T(8,128)(2,1)} %get-tuple-element.213, s32[]{:T(128)S(6)} %select_n.23), kind=kOutput, calls=%fused_computation.4.clone.1 | convolution fusion | flops 137363456 | bytes 3735556 | tf_op jit(solution)/shard_map/while/body/eval_jaxpr/dot_general | solution.py:34
  144.1 2.8 %multiply_convert_fusion.3 = bf16[2048,256]{1,0:T(8,128)(2,1)} fusion(f32[2048,256]{1,0:T(8,128)S(1)} %get-tuple-element.215, bf16[128,256]{1,0:T(8,128)(2,1)S(1)} %get-tuple-element.214, bf16[2048,2048]{1,0:T(8,128)(2,1)} %get-tuple-element.213, s32[]{:T(128)S(6)} %select_n.23), kind=kOutput, calls=%fused_computation.4.clone.1 | convolution fusion | flops 137363456 | bytes 3735556 | tf_op jit(solution)/shard_map/while/body/eval_jaxpr/dot_general | solution.py:34
  150.4 2.8 %multiply_convert_fusion.3 = bf16[2048,256]{1,0:T(8,128)(2,1)} fusion(f32[2048,256]{1,0:T(8,128)S(1)} %get-tuple-element.215, bf16[128,256]{1,0:T(8,128)(2,1)S(1)} %get-tuple-element.214, bf16[2048,2048]{1,0:T(8,128)(2,1)} %get-tuple-element.213, s32[]{:T(128)S(6)} %select_n.23), kind=kOutput, calls=%fused_computation.4.clone.1 | convolution fusion | flops 137363456 | bytes 3735556 | tf_op jit(solution)/shard_map/while/body/eval_jaxpr/dot_general | solution.py:34
  156.7 2.8 %multiply_convert_fusion.3 = bf16[2048,256]{1,0:T(8,128)(2,1)} fusion(f32[2048,256]{1,0:T(8,128)S(1)} %get-tuple-element.215, bf16[128,256]{1,0:T(8,128)(2,1)S(1)} %get-tuple-element.214, bf16[2048,2048]{1,0:T(8,128)(2,1)} %get-tuple-element.213, s32[]{:T(128)S(6)} %select_n.23), kind=kOutput, calls=%fused_computation.4.clone.1 | convolution fusion | flops 137363456 | bytes 3735556 | tf_op jit(solution)/shard_map/while/body/eval_jaxpr/dot_general | solution.py:34
  165.3 39.0 %all-reduce.1 = (f32[2048]{0:T(1024)}, f32[]{:T(128)}) all-reduce(f32[2048]{0:T(1024)S(1)} %neg.21, f32[]{:T(128)S(6)} %neg.22), channel_id=1, replica_groups=mesh['mkt'=8,'trade'=1,'scen'=4] {'mkt','scen'}, use_global_device_ids=true, to_apply=%region_3.4 | all-reduce | flops 2049 | bytes 16392 | tf_op jit(solution)/shard_map/psum | solution.py:47
  (140 shorter events, 80.2 us)
Async XLA Ops:
  0.6 33.4 %copy-start = (bf16[16,128,128]{2,1,0:T(8,128)(2,1)S(1)}, bf16[16,128,128]{2,1,0:T(8,128)(2,1)}, u32[]{:S(2)}) copy-start(bf16[16,128,128]{2,1,0:T(8,128)(2,1)} %param.13) | copy-start | bytes 1572868
  34.4 8.9 %copy-start.2 = (s32[2048]{0:T(1024)S(1)}, s32[2048]{0:T(1024)}, u32[]{:S(2)}) copy-start(s32[2048]{0:T(1024)} %param.14) | copy-start | bytes 24580
  35.2 14.9 %all-to-all-start = ((bf16[16,4,2048]{2,0,1:T(8,128)(2,1)}), bf16[16,4,2048]{2,0,1:T(8,128)(2,1)S(1)}, u32[]{:S(2)}, u32[]{:S(2)}) async-start(bf16[16,4,2048]{2,0,1:T(8,128)(2,1)} %copy.14), calls=%async_computation | async-start | bytes 524288 | tf_op jit(solution)/shard_map/all_to_all | solution.py:26
  50.1 11.0 %copy-start.4 = (bf16[256,256]{1,0:T(8,128)(2,1)S(1)}, bf16[256,256]{1,0:T(8,128)(2,1)}, u32[]{:S(2)}) copy-start(bf16[256,256]{1,0:T(8,128)(2,1)} %param.19) | copy-start | bytes 393220
  50.1 11.0 %copy-start.5 = (bf16[128,256]{1,0:T(8,128)(2,1)S(1)}, bf16[128,256]{1,0:T(8,128)(2,1)}, u32[]{:S(2)}) copy-start(bf16[128,256]{1,0:T(8,128)(2,1)} %param.18) | copy-start | bytes 196612
  50.1 11.0 %copy-start.6 = (f32[256]{0:T(256)S(1)}, f32[256]{0:T(256)}, u32[]{:S(2)}) copy-start(f32[256]{0:T(256)} %param.20) | copy-start | bytes 3076
  50.2 11.0 %copy-start.7 = (bf16[256]{0:T(256)(128)(2,1)S(1)}, bf16[256]{0:T(256)(128)(2,1)}, u32[]{:S(2)}) copy-start(bf16[256]{0:T(256)(128)(2,1)} %param.21) | copy-start | bytes 1540
  61.1 100.6 %copy-start.3 = (s32[16]{0:T(128)S(1)}, s32[16]{0:T(128)}, u32[]{:S(2)}) copy-start(s32[16]{0:T(128)} %param.17) | copy-start | bytes 196
  61.2 101.4 %copy-start.1 = (f32[2048]{0:T(1024)S(1)}, f32[2048]{0:T(1024)}, u32[]{:S(2)}) copy-start(f32[2048]{0:T(1024)} %param.16) | copy-start | bytes 24580
where the time goes:
time: 207 us; the launch traced here: 204 us
  matrix products  80.6 us (39%)
  local copies, waits for them, and re-layouts  57.4 us (28%)
  blocking collectives  39 us (19%)
  loops' own time  10.9 us (5%)
  waiting for transfers between devices  6.9 us (3%)
  starting transfers between devices  6.02 us (3%)
    dot_general x16, matrix products, price(): jnp.dot(trade_rows, w_in, preferred_element_type=jnp.float32) + embed_float  44.7 us
    psum x1, blocking collectives, local(): lax.psum(-jnp.dot(weights, values, precision=lax.Precision.HIGHEST), ('mk...  39 us
    gather x48, local copies, waits for them, and re-layouts  33.3 us
    dot_general x16, matrix products, price(): return jnp.dot(hidden_two, w_out, preferred_element_type=jnp.float32)  32.7 us
    gather x1, local copies, waits for them, and re-layouts, local(): trade_rows_all = table[trade_block]  11 us
    another operation x1, loops' own time, local(): values = lax.map(price, jnp.arange(scen_count, dtype=jnp.int32))  10.9 us
    dynamic_slice x16, local copies, waits for them, and re-layouts, local(): values = lax.map(price, jnp.arange(scen_count, dtype=jnp.int32))  9.38 us
    all_to_all x1, waiting for transfers between devices, local(): lax.all_to_all(built_state, 'scen', split_axis=1, concat_axis=0, tiled=True)  6.9 us
  transfers between devices with their start and end apart: 1, of which 1 were waited for; matrix products, arithmetic and copies ran while one was open for 1% of the time, Pallas kernels for 0%

commit v1 on v0

--- a/solution.py
+++ b/solution.py
@@ -44,7 +44,8 @@
     weight_sum = jnp.sum(jnp.exp(-jnp.arange(scen_total, dtype=jnp.float32) / decay_span))
     weights = jnp.exp(-scen_rank.astype(jnp.float32) / decay_span) / weight_sum
     pnl_part = jnp.dot(values, position, precision=lax.Precision.HIGHEST)
-    marginal = lax.psum(-jnp.dot(weights, values, precision=lax.Precision.HIGHEST), ("mkt", "scen"))
+    z = -jnp.dot(weights, values, precision=lax.Precision.HIGHEST)
+    marginal = jnp.sum(jax.lax.all_gather(z, ("mkt", "scen")), 0)
     book_pnl = lax.psum(pnl_part, "trade")
     local_tail = -jnp.dot(weights, book_pnl, precision=lax.Precision.HIGHEST)
     shortfall = lax.psum(local_tail, ("mkt", "scen"))

time: 207 us -> 276 us (1.33)
  blocking collectives: 39 us -> 106 us
    all_gather x0 -> x1, blocking collectives: none -> 67.7 us  [local(): marginal = jnp.sum(jax.lax.all_gather(z, ('mkt', 'scen')), 0)]
where the time goes in v1:
time: 276 us; the launch traced here: 273 us
  blocking collectives  106 us (38%)
  matrix products  80.7 us (29%)
  local copies, waits for them, and re-layouts  57.4 us (21%)
  loops' own time  10.9 us (4%)
  waiting for transfers between devices  6.9 us (2%)
  starting transfers between devices  6.02 us (2%)
    all_gather x1, blocking collectives, local(): marginal = jnp.sum(jax.lax.all_gather(z, ('mkt', 'scen')), 0)  67.7 us
    dot_general x16, matrix products, price(): jnp.dot(trade_rows, w_in, preferred_element_type=jnp.float32) + embed_float  44.8 us
    psum x1, blocking collectives, local(): shortfall = lax.psum(local_tail, ('mkt', 'scen'))  38.8 us
    gather x48, local copies, waits for them, and re-layouts  33.3 us
    dot_general x16, matrix products, price(): return jnp.dot(hidden_two, w_out, preferred_element_type=jnp.float32)  32.7 us
    gather x1, local copies, waits for them, and re-layouts, local(): trade_rows_all = table[trade_block]  10.9 us
    another operation x1, loops' own time, local(): values = lax.map(price, jnp.arange(scen_count, dtype=jnp.int32))  10.9 us
    dynamic_slice x16, local copies, waits for them, and re-layouts, local(): values = lax.map(price, jnp.arange(scen_count, dtype=jnp.int32))  9.38 us
  transfers between devices with their start and end apart: 1, of which 1 were waited for; matrix products, arithmetic and copies ran while one was open for 1% of the time, Pallas kernels for 0%

profile of v1, /device:TPU:0, one launch (start us, length us, event | category | flops | bytes accessed | tf_op | source)
XLA Modules:
  0.0 272.5 jit_solution(18367021411751131644)
XLA Ops:
  0.7 33.3 %while.12 = (s32[]{:T(128)}, bf16[64,512]{1,0:T(8,128)(2,1)}, s32[16,2]{0,1:T(2,128)S(1)}, bf16[16,64,128]{2,1,0:T(8,128)(2,1)S(1)}, s32[]{:T(128)}) while((s32[]{:T(128)}, bf16[64,512]{1,0:T(8,128)(2,1)}, s32[16,2]{0,1:T(2,128)S(1)}, bf16[16,64,128]{2,1,0:T(8,128)(2,1)S(1)}, s32[]{:T(128)}) %tuple.34), condition=%wide.while_cond, body=%wide.while_body.sunk | while | flops 2 | bytes 32865 | solution.py:20
  35.2 6.0 %all-to-all-start = ((bf16[16,4,2048]{2,0,1:T(8,128)(2,1)}), bf16[16,4,2048]{2,0,1:T(8,128)(2,1)S(1)}, u32[]{:S(2)}, u32[]{:S(2)}) async-start(bf16[16,4,2048]{2,0,1:T(8,128)(2,1)} %copy.15), calls=%async_computation | async-start | bytes 524288 | tf_op jit(solution)/shard_map/all_to_all | solution.py:26
  43.2 6.9 %all-to-all-done = bf16[16,4,2048]{2,0,1:T(8,128)(2,1)S(1)} async-done(((bf16[16,4,2048]{2,0,1:T(8,128)(2,1)}), bf16[16,4,2048]{2,0,1:T(8,128)(2,1)S(1)}, u32[]{:S(2)}, u32[]{:S(2)}) %all-to-all-start) | async-done | bytes 262176 | tf_op jit(solution)/shard_map/all_to_all | solution.py:26
  50.1 10.9 %gather_fusion = bf16[2048,2048]{1,0:T(8,128)(2,1)} fusion(bf16[64,2048]{1,0:T(8,128)(2,1)S(1)} %bitcast.38, s32[2048]{0:T(1024)S(1)} %fusion.6), kind=kCustom, calls=%fused_computation | custom fusion | bytes 16785408 | tf_op jit(solution)/shard_map/gather | solution.py:28
  61.1 100.6 %while.11 = (s32[]{:T(128)}, f32[16,2048]{1,0:T(8,128)S(1)}, s32[16]{0:T(128)S(1)}, bf16[2048,2048]{1,0:T(8,128)(2,1)}, bf16[128,256]{1,0:T(8,128)(2,1)S(1)}, /*...) while((s32[]{:T(128)}, f32[16,2048]{1,0:T(8,128)S(1)}, ...), condition=%wide.region_1.2_spmd, body=%wide.region_0.1_spmd.sunk | while | flops 409993216 | bytes 4942527 | solution.py:41
  62.4 2.8 %multiply_convert_fusion.3 = bf16[2048,256]{1,0:T(8,128)(2,1)} fusion(f32[2048,256]{1,0:T(8,128)S(1)} %get-tuple-element.213, bf16[128,256]{1,0:T(8,128)(2,1)S(1)} %get-tuple-element.212, bf16[2048,2048]{1,0:T(8,128)(2,1)} %get-tuple-element.211, s32[]{:T(128)S(6)} %select_n.23), kind=kOutput, calls=%fused_computation.4.clone.1 | convolution fusion | flops 137363456 | bytes 3735556 | tf_op jit(solution)/shard_map/while/body/eval_jaxpr/dot_general | solution.py:34
  65.2 2.0 fusion.29
  68.7 2.8 %multiply_convert_fusion.3 = bf16[2048,256]{1,0:T(8,128)(2,1)} fusion(f32[2048,256]{1,0:T(8,128)S(1)} %get-tuple-element.213, bf16[128,256]{1,0:T(8,128)(2,1)S(1)} %get-tuple-element.212, bf16[2048,2048]{1,0:T(8,128)(2,1)} %get-tuple-element.211, s32[]{:T(128)S(6)} %select_n.23), kind=kOutput, calls=%fused_computation.4.clone.1 | convolution fusion | flops 137363456 | bytes 3735556 | tf_op jit(solution)/shard_map/while/body/eval_jaxpr/dot_general | solution.py:34
  75.0 2.8 %multiply_convert_fusion.3 = bf16[2048,256]{1,0:T(8,128)(2,1)} fusion(f32[2048,256]{1,0:T(8,128)S(1)} %get-tuple-element.213, bf16[128,256]{1,0:T(8,128)(2,1)S(1)} %get-tuple-element.212, bf16[2048,2048]{1,0:T(8,128)(2,1)} %get-tuple-element.211, s32[]{:T(128)S(6)} %select_n.23), kind=kOutput, calls=%fused_computation.4.clone.1 | convolution fusion | flops 137363456 | bytes 3735556 | tf_op jit(solution)/shard_map/while/body/eval_jaxpr/dot_general | solution.py:34
  81.3 2.8 %multiply_convert_fusion.3 = bf16[2048,256]{1,0:T(8,128)(2,1)} fusion(f32[2048,256]{1,0:T(8,128)S(1)} %get-tuple-element.213, bf16[128,256]{1,0:T(8,128)(2,1)S(1)} %get-tuple-element.212, bf16[2048,2048]{1,0:T(8,128)(2,1)} %get-tuple-element.211, s32[]{:T(128)S(6)} %select_n.23), kind=kOutput, calls=%fused_computation.4.clone.1 | convolution fusion | flops 137363456 | bytes 3735556 | tf_op jit(solution)/shard_map/while/body/eval_jaxpr/dot_general | solution.py:34
  87.6 2.8 %multiply_convert_fusion.3 = bf16[2048,256]{1,0:T(8,128)(2,1)} fusion(f32[2048,256]{1,0:T(8,128)S(1)} %get-tuple-element.213, bf16[128,256]{1,0:T(8,128)(2,1)S(1)} %get-tuple-element.212, bf16[2048,2048]{1,0:T(8,128)(2,1)} %get-tuple-element.211, s32[]{:T(128)S(6)} %select_n.23), kind=kOutput, calls=%fused_computation.4.clone.1 | convolution fusion | flops 137363456 | bytes 3735556 | tf_op jit(solution)/shard_map/while/body/eval_jaxpr/dot_general | solution.py:34
  93.8 2.8 %multiply_convert_fusion.3 = bf16[2048,256]{1,0:T(8,128)(2,1)} fusion(f32[2048,256]{1,0:T(8,128)S(1)} %get-tuple-element.213, bf16[128,256]{1,0:T(8,128)(2,1)S(1)} %get-tuple-element.212, bf16[2048,2048]{1,0:T(8,128)(2,1)} %get-tuple-element.211, s32[]{:T(128)S(6)} %select_n.23), kind=kOutput, calls=%fused_computation.4.clone.1 | convolution fusion | flops 137363456 | bytes 3735556 | tf_op jit(solution)/shard_map/while/body/eval_jaxpr/dot_general | solution.py:34
  100.1 2.8 %multiply_convert_fusion.3 = bf16[2048,256]{1,0:T(8,128)(2,1)} fusion(f32[2048,256]{1,0:T(8,128)S(1)} %get-tuple-element.213, bf16[128,256]{1,0:T(8,128)(2,1)S(1)} %get-tuple-element.212, bf16[2048,2048]{1,0:T(8,128)(2,1)} %get-tuple-element.211, s32[]{:T(128)S(6)} %select_n.23), kind=kOutput, calls=%fused_computation.4.clone.1 | convolution fusion | flops 137363456 | bytes 3735556 | tf_op jit(solution)/shard_map/while/body/eval_jaxpr/dot_general | solution.py:34
  106.4 2.8 %multiply_convert_fusion.3 = bf16[2048,256]{1,0:T(8,128)(2,1)} fusion(f32[2048,256]{1,0:T(8,128)S(1)} %get-tuple-element.213, bf16[128,256]{1,0:T(8,128)(2,1)S(1)} %get-tuple-element.212, bf16[2048,2048]{1,0:T(8,128)(2,1)} %get-tuple-element.211, s32[]{:T(128)S(6)} %select_n.23), kind=kOutput, calls=%fused_computation.4.clone.1 | convolution fusion | flops 137363456 | bytes 3735556 | tf_op jit(solution)/shard_map/while/body/eval_jaxpr/dot_general | solution.py:34
  112.7 2.8 %multiply_convert_fusion.3 = bf16[2048,256]{1,0:T(8,128)(2,1)} fusion(f32[2048,256]{1,0:T(8,128)S(1)} %get-tuple-element.213, bf16[128,256]{1,0:T(8,128)(2,1)S(1)} %get-tuple-element.212, bf16[2048,2048]{1,0:T(8,128)(2,1)} %get-tuple-element.211, s32[]{:T(128)S(6)} %select_n.23), kind=kOutput, calls=%fused_computation.4.clone.1 | convolution fusion | flops 137363456 | bytes 3735556 | tf_op jit(solution)/shard_map/while/body/eval_jaxpr/dot_general | solution.py:34
  119.0 2.8 %multiply_convert_fusion.3 = bf16[2048,256]{1,0:T(8,128)(2,1)} fusion(f32[2048,256]{1,0:T(8,128)S(1)} %get-tuple-element.213, bf16[128,256]{1,0:T(8,128)(2,1)S(1)} %get-tuple-element.212, bf16[2048,2048]{1,0:T(8,128)(2,1)} %get-tuple-element.211, s32[]{:T(128)S(6)} %select_n.23), kind=kOutput, calls=%fused_computation.4.clone.1 | convolution fusion | flops 137363456 | bytes 3735556 | tf_op jit(solution)/shard_map/while/body/eval_jaxpr/dot_general | solution.py:34
  125.3 2.8 %multiply_convert_fusion.3 = bf16[2048,256]{1,0:T(8,128)(2,1)} fusion(f32[2048,256]{1,0:T(8,128)S(1)} %get-tuple-element.213, bf16[128,256]{1,0:T(8,128)(2,1)S(1)} %get-tuple-element.212, bf16[2048,2048]{1,0:T(8,128)(2,1)} %get-tuple-element.211, s32[]{:T(128)S(6)} %select_n.23), kind=kOutput, calls=%fused_computation.4.clone.1 | convolution fusion | flops 137363456 | bytes 3735556 | tf_op jit(solution)/shard_map/while/body/eval_jaxpr/dot_general | solution.py:34
  131.6 2.8 %multiply_convert_fusion.3 = bf16[2048,256]{1,0:T(8,128)(2,1)} fusion(f32[2048,256]{1,0:T(8,128)S(1)} %get-tuple-element.213, bf16[128,256]{1,0:T(8,128)(2,1)S(1)} %get-tuple-element.212, bf16[2048,2048]{1,0:T(8,128)(2,1)} %get-tuple-element.211, s32[]{:T(128)S(6)} %select_n.23), kind=kOutput, calls=%fused_computation.4.clone.1 | convolution fusion | flops 137363456 | bytes 3735556 | tf_op jit(solution)/shard_map/while/body/eval_jaxpr/dot_general | solution.py:34
  137.9 2.8 %multiply_convert_fusion.3 = bf16[2048,256]{1,0:T(8,128)(2,1)} fusion(f32[2048,256]{1,0:T(8,128)S(1)} %get-tuple-element.213, bf16[128,256]{1,0:T(8,128)(2,1)S(1)} %get-tuple-element.212, bf16[2048,2048]{1,0:T(8,128)(2,1)} %get-tuple-element.211, s32[]{:T(128)S(6)} %select_n.23), kind=kOutput, calls=%fused_computation.4.clone.1 | convolution fusion | flops 137363456 | bytes 3735556 | tf_op jit(solution)/shard_map/while/body/eval_jaxpr/dot_general | solution.py:34
  144.2 2.8 %multiply_convert_fusion.3 = bf16[2048,256]{1,0:T(8,128)(2,1)} fusion(f32[2048,256]{1,0:T(8,128)S(1)} %get-tuple-element.213, bf16[128,256]{1,0:T(8,128)(2,1)S(1)} %get-tuple-element.212, bf16[2048,2048]{1,0:T(8,128)(2,1)} %get-tuple-element.211, s32[]{:T(128)S(6)} %select_n.23), kind=kOutput, calls=%fused_computation.4.clone.1 | convolution fusion | flops 137363456 | bytes 3735556 | tf_op jit(solution)/shard_map/while/body/eval_jaxpr/dot_general | solution.py:34
  150.5 2.8 %multiply_convert_fusion.3 = bf16[2048,256]{1,0:T(8,128)(2,1)} fusion(f32[2048,256]{1,0:T(8,128)S(1)} %get-tuple-element.213, bf16[128,256]{1,0:T(8,128)(2,1)S(1)} %get-tuple-element.212, bf16[2048,2048]{1,0:T(8,128)(2,1)} %get-tuple-element.211, s32[]{:T(128)S(6)} %select_n.23), kind=kOutput, calls=%fused_computation.4.clone.1 | convolution fusion | flops 137363456 | bytes 3735556 | tf_op jit(solution)/shard_map/while/body/eval_jaxpr/dot_general | solution.py:34
  156.8 2.8 %multiply_convert_fusion.3 = bf16[2048,256]{1,0:T(8,128)(2,1)} fusion(f32[2048,256]{1,0:T(8,128)S(1)} %get-tuple-element.213, bf16[128,256]{1,0:T(8,128)(2,1)S(1)} %get-tuple-element.212, bf16[2048,2048]{1,0:T(8,128)(2,1)} %get-tuple-element.211, s32[]{:T(128)S(6)} %select_n.23), kind=kOutput, calls=%fused_computation.4.clone.1 | convolution fusion | flops 137363456 | bytes 3735556 | tf_op jit(solution)/shard_map/while/body/eval_jaxpr/dot_general | solution.py:34
  165.3 38.8 %psum.6 = f32[]{:T(128)} all-reduce(f32[]{:T(128)S(6)} %neg.22), channel_id=1, replica_groups=mesh['mkt'=8,'trade'=1,'scen'=4] {'mkt','scen'}, use_global_device_ids=true, to_apply=%region_4.5 | all-reduce | flops 1 | bytes 8 | tf_op jit(solution)/shard_map/psum | solution.py:51
  204.2 67.7 %all-gather = f32[65536]{0:T(1024)S(1)} all-gather(f32[2048]{0:T(1024)S(1)} %neg.21), channel_id=2, replica_groups=mesh['mkt'=8,'trade'=1,'scen'=4] {'mkt','scen'}, dimensions={0}, use_global_device_ids=true | all-gather | bytes 270336 | tf_op jit(solution)/shard_map/all_gather | solution.py:48
  (143 shorter events, 82.9 us)
Async XLA Ops:
  0.6 33.4 %copy-start = (bf16[16,128,128]{2,1,0:T(8,128)(2,1)S(1)}, bf16[16,128,128]{2,1,0:T(8,128)(2,1)}, u32[]{:S(2)}) copy-start(bf16[16,128,128]{2,1,0:T(8,128)(2,1)} %param.13) | copy-start | bytes 1572868
  34.4 8.9 %copy-start.2 = (s32[2048]{0:T(1024)S(1)}, s32[2048]{0:T(1024)}, u32[]{:S(2)}) copy-start(s32[2048]{0:T(1024)} %param.14) | copy-start | bytes 24580
  35.2 14.9 %all-to-all-start = ((bf16[16,4,2048]{2,0,1:T(8,128)(2,1)}), bf16[16,4,2048]{2,0,1:T(8,128)(2,1)S(1)}, u32[]{:S(2)}, u32[]{:S(2)}) async-start(bf16[16,4,2048]{2,0,1:T(8,128)(2,1)} %copy.15), calls=%async_computation | async-start | bytes 524288 | tf_op jit(solution)/shard_map/all_to_all | solution.py:26
  50.1 11.0 %copy-start.4 = (bf16[256,256]{1,0:T(8,128)(2,1)S(1)}, bf16[256,256]{1,0:T(8,128)(2,1)}, u32[]{:S(2)}) copy-start(bf16[256,256]{1,0:T(8,128)(2,1)} %param.19) | copy-start | bytes 393220
  50.1 11.0 %copy-start.5 = (bf16[128,256]{1,0:T(8,128)(2,1)S(1)}, bf16[128,256]{1,0:T(8,128)(2,1)}, u32[]{:S(2)}) copy-start(bf16[128,256]{1,0:T(8,128)(2,1)} %param.18) | copy-start | bytes 196612
  50.1 11.0 %copy-start.6 = (f32[256]{0:T(256)S(1)}, f32[256]{0:T(256)}, u32[]{:S(2)}) copy-start(f32[256]{0:T(256)} %param.20) | copy-start | bytes 3076
  50.1 11.0 %copy-start.7 = (bf16[256]{0:T(256)(128)(2,1)S(1)}, bf16[256]{0:T(256)(128)(2,1)}, u32[]{:S(2)}) copy-start(bf16[256]{0:T(256)(128)(2,1)} %param.21) | copy-start | bytes 1540
  61.1 100.7 %copy-start.1 = (f32[2048]{0:T(1024)S(1)}, f32[2048]{0:T(1024)}, u32[]{:S(2)}) copy-start(f32[2048]{0:T(1024)} %param.16) | copy-start | bytes 24580
  61.1 100.7 %copy-start.3 = (s32[16]{0:T(128)S(1)}, s32[16]{0:T(128)}, u32[]{:S(2)}) copy-start(s32[16]{0:T(128)} %param.17) | copy-start | bytes 196
